TPU v7x, 32 devices: a whole 2x2x4 slice. The times are simulated.
32 devices in a mesh: gx: 4 (over y, core), yz: 8 (over z, x).
Axes of the slice: x: 2, y: 2, z: 4, core: 2. Of those that a mesh axis runs over, the one named last changes fastest.
Arguments:
- gas_state: float32 [5, 64, 128, 256], P(None, 'gx', 'yz'), may hold values from -6 to 6
- parcel_speed: float32 [4, 8, 32, 4, 3, 128], P('gx', 'yz'), may hold values from -6 to 6
- parcel_mass: float32 [4, 8, 32, 4, 128], P('gx', 'yz'), may hold values from 0.3 to 3
- offsets: float32 [4, 8, 32, 4, 3, 128], P('gx', 'yz'), may hold values from 0 to 1
- cell_base: int32 [4, 8, 32, 4, 3, 128], P('gx', 'yz'), may hold values from 0 to 6, as said below
- block_tile: int32 [4, 8, 32, 4], P('gx', 'yz'), may hold values from 0 to 511
- block_count: int32 [4, 8, 32], P('gx', 'yz'), may hold values from 0 to 4, as said below
Outputs:
- gas_next: float32 [5, 64, 128, 256], P(None, 'gx', 'yz')
- speed_next: float32 [4, 8, 32, 4, 3, 128], P('gx', 'yz')
- mass_next: float32 [4, 8, 32, 4, 128], P('gx', 'yz')
Inputs may be any that keep to these rules, and one draw needn't show every extreme that they name: `block_count`: A device's live blocks for an owner are its first ones; in every draw some owner receives 4 live blocks from every device. `cell_base`: component 0, 1, 2 is at most 2, 2, 6, so that the base cell and the next cell along each dimension lie in the tile.
All inputs are finite; a program needn't handle non-finite values.
Results may differ from a plain program's by a relative error of at most 0.0003.
Values sent between devices are 32-bit elements; how exact they have to be, the bound alone decides.
No kernel may reach another device: no remote copies, remote signals or barrier semaphores. Data moves between devices by JAX's collectives and lax.ppermute only.
A program may use at most 128 MiB of HBM per device.

v0:
```python
import functools

import jax
import jax.numpy as jnp
from jax import lax
from jax.experimental import pallas as pl
from jax.experimental.pallas import tpu as pltpu
from jax.sharding import PartitionSpec as P


TILE_X = 4
TILE_Y = 4
TILE_Z = 8
DIFFUSION = 0.1
CELL_MASS = 4.0
DRAG_RATE = 0.5
EVAPORATION = 0.3
LATENT_HEAT = 2.0

LANES = 128
SUB = 8
GRANULES = LANES // TILE_Z
FLOWS = 4
SENT = ("yz", "gx")
RETURNED = ("gx", "yz")


def roll(x, shift, axis):
    shift = shift % x.shape[axis]
    return pltpu.roll(x, shift, axis) if shift else x


def pick(x, rows):
    return jnp.take_along_axis(x, rows, axis=0, mode="promise_in_bounds")


def exchange(upper, lower):
    row = lax.broadcasted_iota(jnp.int32, (SUB, LANES), 0)
    granule = lax.broadcasted_iota(jnp.int32, (SUB, LANES), 1) // TILE_Z
    half = LANES // 2
    turned = [
        pltpu.roll(x, shift, 1, stride=TILE_Z, stride_axis=0) for x, shift in ((upper, 0), (lower, half))
    ]
    back = SUB - 1 - row
    pair = []
    for part in range(2):
        wanted = (granule - back - SUB * part) % GRANULES
        mixed = jnp.where(wanted < SUB, pick(turned[0], wanted % SUB), pick(turned[1], wanted % SUB))
        shift = (-TILE_Z * (SUB - 1) - half * part) % LANES
        pair.append(pick(pltpu.roll(mixed, shift, 1, stride=TILE_Z, stride_axis=0), back))
    return pair


def pack_kernel(
    speed, mass, offsets, cells, tile_ids, counts, message,
    speed_v, mass_v, offsets_v, cells_v, tile_ids_v, counts_v, message_v, sems, *, rows, capacity, parts
):
    across_i = speed.shape[0]
    vector = 3 * capacity
    across_j = speed.shape[1] // vector
    each = across_j // parts
    sources = ((speed, speed_v, vector), (offsets, offsets_v, vector), (cells, cells_v, vector), (mass, mass_v, capacity))
    small = [
        pltpu.make_async_copy(tile_ids, tile_ids_v, sems.at[0]),
        pltpu.make_async_copy(counts, counts_v, sems.at[1]),
    ]
    taken = []
    for copy in small:
        copy.start()
    for part in range(parts):
        taken.append([])
        for n, (source, held, count) in enumerate(sources):
            place = pl.ds(part * each * count, each * count)
            copy = pltpu.make_async_copy(source.at[:, place], held.at[:, place], sems.at[2 + part * 5 + n])
            copy.start()
            taken[-1].append(copy)
    sent = []
    for part in range(parts):
        for copy in taken[part]:
            copy.wait()
        if part == 0:
            for copy in small:
                copy.wait()
            slot = lax.broadcasted_iota(jnp.int32, tile_ids_v.shape, 0)
            ids = jnp.where(slot < counts_v[...], tile_ids_v[...], -1).astype(jnp.float32)
            ids = jnp.concatenate([ids, jnp.zeros((LANES - capacity, ids.shape[1]), jnp.float32)], axis=0).T
        for j in range(part * each, (part + 1) * each):
            for i in range(across_i):
                base = (j * across_i + i) * rows
                place = slice(j * vector, (j + 1) * vector)
                message_v[base : base + vector, :] = speed_v[i, place, :]
                message_v[base + vector : base + 2 * vector, :] = offsets_v[i, place, :]
                message_v[base + 2 * vector : base + 3 * vector, :] = cells_v[i, place, :].astype(jnp.float32)
                base += 3 * vector
                message_v[base : base + capacity, :] = mass_v[i, j * capacity : (j + 1) * capacity, :]
                owner = i * across_j + j
                message_v[base + capacity : base + capacity + 1, :] = ids[owner : owner + 1, :]
        place = pl.ds(part * each * across_i * rows, each * across_i * rows)
        copy = pltpu.make_async_copy(message_v.at[place], message.at[place], sems.at[2 + part * 5 + 4])
        copy.start()
        sent.append(copy)
    for copy in sent:
        copy.wait()


def table_kernel(gas_hbm, table, face_x0, face_x1, face_y0, face_y1, gas, sem):
    copy = pltpu.make_async_copy(gas_hbm, gas, sem)
    copy.start()
    copy.wait()
    extent_x, extent_y, extent_z = gas.shape[1:]
    across_y = extent_y // TILE_Y
    across_z = extent_z // TILE_Z
    face_x0[...] = gas[:, 0]
    face_x1[...] = gas[:, extent_x - 1]
    face_y0[...] = gas[:, :, 0, :]
    face_y1[...] = gas[:, :, extent_y - 1, :]

    def per_a(a, carry):
        for f in range(FLOWS):
            for b in range(across_y):
                for h in range(extent_z // LANES):
                    lanes = slice(h * LANES, (h + 1) * LANES)
                    rows = slice(b * TILE_Y, (b + 1) * TILE_Y)
                    parts = []
                    for u in range(TILE_X):
                        piece = gas[f, a * TILE_X + u, rows, lanes]
                        if f == 3:
                            piece = piece - gas[4, a * TILE_X + u, rows, lanes]
                        parts.append(piece)
                    pair = exchange(jnp.concatenate(parts[:2], 0), jnp.concatenate(parts[2:], 0))
                    start = pl.multiple_of((a * across_y + b) * across_z + h * GRANULES, SUB)
                    table[f, pl.ds(start, SUB), :] = pair[0]
                    table[f, pl.ds(start + SUB, SUB), :] = pair[1]
        return carry

    lax.fori_loop(0, extent_x // TILE_X, per_a, 0)


def paired(ref, member, stride, offset, capacity):
    starts = [(member + n) * stride + offset for n in range(2)]
    return jnp.concatenate([ref[start : start + capacity, :] for start in starts], axis=0)


def columns(g, across_i, spread):
    size = SUB // across_i * spread
    return pl.ds(pl.multiple_of(g * size, SUB), size)


def update_kernel(
    message, table, result_hbm, result, ids_vmem, turned, sems, *, rows, capacity
):
    devices = message.shape[0] // rows
    group = SUB * rows
    for g in range(devices // SUB):
        ids_vmem[g * SUB : (g + 1) * SUB, :] = message[pl.ds(g * group + rows - 1, SUB, stride=rows), :].astype(jnp.int32)
    for k in range(capacity):
        turned[k] = roll(ids_vmem[...], -k, 1)
    corner = lax.broadcasted_iota(jnp.int32, (SUB, LANES), 0)
    high = [(corner & bit) != 0 for bit in (4, 2, 1)]
    least = [jnp.where(h, 0.0, 1.0) for h in high]
    slope = [jnp.where(h, 1.0, -1.0) for h in high]
    shift = (
        jnp.where(high[0], TILE_Y * TILE_Z, 0) + jnp.where(high[1], TILE_Z, 0) + jnp.where(high[2], 1, 0)
    )
    row = corner

    across_i = result.shape[0]
    spread = capacity * FLOWS

    def returned(g):
        place = columns(g, across_i, spread)
        return pltpu.make_async_copy(result.at[:, place], result_hbm.at[:, place], sems.at[g])

    def per_group(g, carry):
        out = result.at[:, columns(g, across_i, spread)]
        here = pl.ds(pl.multiple_of(g * SUB, SUB), SUB)
        numbers = [turned[k, here, :] for k in range(capacity)]
        part = message.at[pl.ds(pl.multiple_of(g * group, SUB), group)]
        for step in range(SUB // 2):

            def both(field):
                return paired(part, 2 * step, rows, field * capacity, capacity)

            first = ((both(6) * TILE_Y + both(7)) * TILE_Z + both(8)).astype(jnp.int32)
            alive = jnp.zeros((SUB, LANES), jnp.int32)
            made = [[] for _ in range(FLOWS)]
            for j in range(2 * capacity):
                i, k = 2 * step + j // capacity, j % capacity
                base = i * rows
                tile = numbers[k][i, 0]
                alive = jnp.where(row == j, tile, alive)
                safe = jnp.maximum(tile, 0)
                weight = None
                for dim in range(3):
                    start = base + (3 + dim) * capacity + k
                    fraction = part[start : start + 1, :]
                    along = least[dim] + slope[dim] * fraction
                    weight = along if weight is None else weight * along
                index = jnp.broadcast_to(first[j : j + 1], (SUB, LANES)) + shift
                for f in range(FLOWS):
                    held = jnp.broadcast_to(table[f, pl.ds(safe, 1), :], (SUB, LANES))
                    found = jnp.take_along_axis(held, index, axis=1, mode="promise_in_bounds")
                    made[f].append(found * weight)
            live = alive >= 0
            sampled = []
            for level in made:
                for size in (4, 2, 1):
                    keep = (row & size) == 0
                    half = len(level) // 2
                    level = [
                        jnp.where(keep, x, roll(y, size, 0)) + jnp.where(keep, roll(x, -size, 0), y)
                        for x, y in zip(level[:half], level[half:])
                    ]
                sampled.append(level[0])

            mass_old = both(9)
            radius = jnp.exp(jnp.log(mass_old) * (1.0 / 3.0))
            factor = DRAG_RATE / (radius * radius)
            share = 1.0 / (1.0 + factor)
            gap = sampled[3]
            soft = jnp.maximum(gap, 0.0) + jnp.log(1.0 + jnp.exp(-jnp.abs(gap)))
            mass_new = jnp.where(live, mass_old / (1.0 + EVAPORATION * soft / radius), mass_old)
            fields = [
                jnp.where(live, (both(f) + factor * sampled[f]) * share, both(f)) for f in range(3)
            ] + [mass_new]
            for n in range(2):
                i, start = (2 * step + n) % across_i, (2 * step + n) // across_i * spread
                for f in range(FLOWS):
                    rows_f = slice(start + f * capacity, start + (f + 1) * capacity)
                    out[i, rows_f, :] = fields[f][n * capacity : (n + 1) * capacity]
        returned(g).start()
        return carry

    lax.fori_loop(0, devices // SUB, per_group, 0, unroll=4)
    for g in range(devices // SUB):
        returned(g).wait()


def tent(position, cell):
    return jnp.maximum(0.0, 1.0 - jnp.abs(position - cell))


def deposit_kernel(
    ids_vmem, message, result, gas_hbm, from_x0, from_x1, from_y0, from_y1, gas_next,
    total, source, ids, gas, work, sems, *, rows, capacity
):
    fields, extent_x, extent_z = from_y0.shape
    extent_y = from_x0.shape[1]
    across_y = extent_y // TILE_Y
    across_z = extent_z // TILE_Z
    blocks = source.shape[0] // SUB
    group = SUB * rows
    spread = capacity * FLOWS
    across_i = result.shape[0]
    copy = pltpu.make_async_copy(ids_vmem, ids, sems.at[0])
    copy.start()
    fetch = pltpu.make_async_copy(gas_hbm, gas, sems.at[1])
    fetch.start()
    total[...] = jnp.zeros(total.shape, total.dtype)

    def per_group(g, carry):
        part = message.at[pl.ds(pl.multiple_of(g * group, SUB), group)]
        updated = result.at[:, columns(g, across_i, spread)]
        out = source.at[pl.ds(pl.multiple_of(g * SUB * SUB * capacity, SUB), SUB * SUB * capacity)]
        for step in range(SUB // 2):

            def before(field):
                return paired(part, 2 * step, rows, field * capacity, capacity)

            def after(field):
                found = []
                for member in (2 * step, 2 * step + 1):
                    i, start = member % across_i, member // across_i * spread + field * capacity
                    found.append(updated[i, start : start + capacity, :])
                return jnp.concatenate(found, axis=0)

            mass_old = before(9)
            vapour = mass_old - after(3)
            found = [mass_old * (before(f) - after(f)) + vapour * after(f) for f in range(3)] + [vapour]
            found += [before(3 + dim) + before(6 + dim) for dim in range(3)]
            for f, value in enumerate(found):
                out[pl.ds(2 * step * capacity * SUB + f, 2 * capacity, stride=SUB), :] = value
        return carry

    lax.fori_loop(0, blocks // (SUB * capacity), per_group, 0)
    row = lax.broadcasted_iota(jnp.int32, (SUB, LANES), 0)
    along_z = row.astype(jnp.float32)
    along_y = (row % TILE_Y).astype(jnp.float32)
    along_x = (row // TILE_Y).astype(jnp.float32)
    copy.wait()

    def one(n):
        tile = jnp.maximum(ids[n // capacity, n % capacity], 0)
        held = source[pl.ds(pl.multiple_of(n * SUB, SUB), SUB), :]
        given = held[0:FLOWS]
        coarse = given.astype(jnp.bfloat16).astype(jnp.float32)
        left = jnp.concatenate([given, given - coarse], axis=0).astype(jnp.bfloat16)
        x, y, z = held[4:5], held[5:6], held[6:7]
        weight_z = tent(z, along_z)
        weight_y = tent(y, along_y)
        planes = []
        for part in range(2):
            weight_xy = tent(x, along_x + 2.0 * part) * weight_y
            for i in range(SUB):
                planes.append(weight_xy[i : i + 1] * weight_z)
        stencil = jnp.concatenate(planes, axis=0)
        high = stencil.astype(jnp.bfloat16)
        low = (stencil - high.astype(jnp.float32)).astype(jnp.bfloat16)
        right = jnp.concatenate([high, low], axis=0)
        sums = lax.dot_general(left, right, (((1,), (1,)), ((), ())), preferred_element_type=jnp.float32)
        return pl.multiple_of(tile * SUB, SUB), sums[:, :LANES] + sums[:, LANES:]

    unroll = 16

    def per_step(step, carry):
        made = [one(step * unroll + n) for n in range(unroll)]
        for start, sums in made:
            total[pl.ds(start, SUB), :] += sums
        return carry

    lax.fori_loop(0, blocks // unroll, per_step, 0)

    fetch.wait()
    lane = lax.broadcasted_iota(jnp.int32, (extent_y, extent_z), 1)
    line = lax.broadcasted_iota(jnp.int32, (extent_y, extent_z), 0)

    def per_field(f, carry):
        for x in range(extent_x):
            centre = gas[f, x]
            beside = from_x0[f] if x == 0 else gas[f, x - 1]
            beside += from_x1[f] if x == extent_x - 1 else gas[f, x + 1]
            beside += jnp.where(line == 0, from_y0[f, x : x + 1, :], roll(centre, 1, 0))
            beside += jnp.where(line == extent_y - 1, from_y1[f, x : x + 1, :], roll(centre, -1, 0))
            beside += jnp.where(lane == 0, 0.0, roll(centre, 1, 1))
            beside += jnp.where(lane == extent_z - 1, 0.0, roll(centre, -1, 1))
            work[f, x * extent_y : (x + 1) * extent_y, :] = centre + DIFFUSION * (beside - 6.0 * centre)
        return carry

    lax.fori_loop(0, fields, per_field, 0)

    def sent(a):
        place = pl.ds(pl.multiple_of(a * TILE_X * extent_y, SUB), TILE_X * extent_y)
        return pltpu.make_async_copy(work.at[:, place], gas_next.at[:, place], sems.at[2 + a])

    def per_a(a, carry):
        held = work.at[:, pl.ds(pl.multiple_of(a * TILE_X * extent_y, SUB), TILE_X * extent_y)]
        for b in range(across_y):
            for h in range(extent_z // LANES):
                start = ((a * across_y + b) * across_z + h * GRANULES) * SUB
                part = total.at[pl.ds(pl.multiple_of(start, SUB), GRANULES * SUB)]
                lanes = slice(h * LANES, (h + 1) * LANES)
                for f in range(FLOWS):
                    pair = [
                        part[pl.ds(n * SUB * SUB + f, SUB, stride=SUB), :]
                        + part[pl.ds(n * SUB * SUB + f + FLOWS, SUB, stride=SUB), :]
                        for n in range(2)
                    ]
                    pair = [x * (1.0 / CELL_MASS) for x in exchange(*pair)]
                    for u in range(TILE_X):
                        piece = pair[u // 2][(u % 2) * TILE_Y : (u % 2 + 1) * TILE_Y]
                        spot = u * extent_y + b * TILE_Y
                        lines = slice(spot, spot + TILE_Y)
                        if f < 3:
                            held[f, lines, lanes] += piece
                        else:
                            held[3, lines, lanes] -= LATENT_HEAT * piece
                            held[4, lines, lanes] += piece
        sent(a).start()
        return carry

    lax.fori_loop(0, extent_x // TILE_X, per_a, 0)
    for a in range(extent_x // TILE_X):
        sent(a).wait()


def unpack_kernel(result, speed, mass, sems):
    vector = speed.shape[1]
    copies = [
        pltpu.make_async_copy(result.at[:, :vector], speed, sems.at[0]),
        pltpu.make_async_copy(result.at[:, vector:], mass, sems.at[1]),
    ]
    for copy in copies:
        copy.start()
    for copy in copies:
        copy.wait()


def specs(spaces):
    return [pl.BlockSpec(memory_space=space) for space in spaces]


def call(kernel, out_shape, scratch=(), flops=0, moved=0, ins=None, outs=None):
    extra = {}
    if ins is not None:
        extra["in_specs"] = specs(ins)
    if outs is not None:
        extra["out_specs"] = specs(outs) if len(outs) > 1 else specs(outs)[0]
        if pltpu.HBM in outs:
            shapes = out_shape if len(outs) > 1 else (out_shape,)
            shapes = [pltpu.HBM(o.shape, o.dtype) if space == pltpu.HBM else o for o, space in zip(shapes, outs)]
            out_shape = shapes if len(outs) > 1 else shapes[0]
    called = pl.pallas_call(
        kernel,
        out_shape=out_shape,
        scratch_shapes=scratch,
        cost_estimate=pl.CostEstimate(flops=flops, bytes_accessed=moved, transcendentals=0),
        compiler_params=pltpu.CompilerParams(vmem_limit_bytes=32 * 1024 * 1024),
        **extra,
    )

    def with_spaces(*values):
        if ins is not None:
            values = [
                pltpu.with_memory_space_constraint(v, space) if space == pltpu.HBM else v
                for v, space in zip(values, ins)
            ]
        return called(*values)

    return with_spaces


def step(gas_state, parcel_speed, parcel_mass, offsets, cell_base, block_tile, block_count):
    fields, extent_x, extent_y, extent_z = gas_state.shape
    devices, capacity = block_tile.shape[2:]
    rows = 10 * capacity + 1
    tiles = (extent_x // TILE_X) * (extent_y // TILE_Y) * (extent_z // TILE_Z)
    f32 = jnp.float32

    def shape(*dims, dtype=f32):
        return jax.ShapeDtypeStruct(dims, dtype)

    vector = 3 * capacity
    blocks = devices * capacity
    across_i, across_j = lax.axis_size("gx"), lax.axis_size("yz")
    parts = max(1, across_j // 2)
    i32 = jnp.int32
    hbm, vmem = pltpu.HBM, pltpu.VMEM
    dma = pltpu.SemaphoreType.DMA

    def by_component(value):
        return value[0, 0].transpose(0, 2, 1, 3).reshape(across_i, across_j * vector, LANES)

    message = call(
        functools.partial(pack_kernel, rows=rows, capacity=capacity, parts=parts),
        shape(devices * rows, LANES),
        scratch=[
            vmem((across_i, across_j * vector, LANES), f32),
            vmem((across_i, across_j * capacity, LANES), f32),
            vmem((across_i, across_j * vector, LANES), f32),
            vmem((across_i, across_j * vector, LANES), i32),
            vmem((capacity, devices), i32),
            vmem((1, devices), i32),
            vmem((devices * rows, LANES), f32),
            dma((2 + 5 * parts,)),
        ],
        ins=[hbm] * 6,
        outs=[hbm],
    )(
        by_component(parcel_speed),
        parcel_mass.reshape(across_i, across_j * capacity, LANES),
        by_component(offsets),
        by_component(cell_base),
        block_tile[0, 0].T,
        block_count[0],
    )
    message = lax.all_to_all(message.reshape(devices, rows, 1, LANES), SENT, split_axis=0, concat_axis=0, tiled=True)
    message = message.reshape(devices * rows, LANES)

    face = shape(fields, extent_x, extent_z)
    side = shape(fields, extent_y, extent_z)
    whole = vmem(gas_state.shape, f32)
    flat = (fields, extent_x * extent_y, extent_z)
    table, face_x0, face_x1, face_y0, face_y1 = call(
        table_kernel,
        (shape(FLOWS, tiles, LANES), side, side, face, face),
        scratch=[whole, dma(())],
        flops=10**7,
        ins=[hbm],
        outs=[vmem] * 5,
    )(gas_state)

    def shifted(value, axis, step):
        count = lax.axis_size(axis)
        pairs = [(i, i + step) for i in range(count) if 0 <= i + step < count]
        return lax.ppermute(value, axis, pairs)

    from_y0 = shifted(face_y1, "yz", 1)
    from_y1 = shifted(face_y0, "yz", -1)
    from_x0 = shifted(face_x1, "gx", 1)
    from_x1 = shifted(face_x0, "gx", -1)
    halo = (from_x0, from_x1, from_y0, from_y1)
    returned, result, ids = call(
        functools.partial(update_kernel, rows=rows, capacity=capacity),
        (
            shape(across_i, across_j * capacity * FLOWS, LANES),
            shape(across_i, across_j * capacity * FLOWS, LANES),
            shape(devices, LANES, dtype=i32),
        ),
        scratch=[
            vmem((capacity, devices, LANES), i32),
            dma((devices // SUB,)),
        ],
        flops=10**7,
        ins=[vmem, vmem],
        outs=[hbm, vmem, vmem],
    )(message, table)
    returned = lax.all_to_all(
        returned.reshape(devices, capacity * FLOWS, 1, LANES), RETURNED, split_axis=0, concat_axis=0, tiled=True
    )
    gas_next = call(
        functools.partial(deposit_kernel, rows=rows, capacity=capacity),
        shape(*flat),
        scratch=[
            vmem((tiles * SUB, LANES), f32),
            vmem((blocks * SUB, LANES), f32),
            pltpu.SMEM((devices, LANES), i32),
            whole,
            vmem(flat, f32),
            dma((2 + extent_x // TILE_X,)),
        ],
        flops=3 * 10**7,
        ins=[vmem, vmem, vmem, hbm] + [vmem] * 4,
        outs=[hbm],
    )(ids, message, result, gas_state, *halo)
    speed_next, mass_next = call(
        unpack_kernel,
        (shape(devices, vector, 1, LANES), shape(devices, capacity, 1, LANES)),
        scratch=[dma((2,))],
        ins=[vmem],
        outs=[hbm, hbm],
    )(returned)
    speed_next = speed_next.reshape(devices, 3, capacity, LANES).transpose(0, 2, 1, 3)
    return gas_next.reshape(gas_state.shape), speed_next.reshape(parcel_speed.shape), mass_next.reshape(parcel_mass.shape)


def solution(mesh):
    in_specs = (
        P(None, "gx", "yz", None),
        P("gx", "yz", None, None, None, None),
        P("gx", "yz", None, None, None),
        P("gx", "yz", None, None, None, None),
        P("gx", "yz", None, None, None, None),
        P("gx", "yz", None, None),
        P("gx", "yz", None),
    )
    out_specs = (
        P(None, "gx", "yz", None),
        P("gx", "yz", None, None, None, None),
        P("gx", "yz", None, None, None),
    )
    return jax.shard_map(step, mesh=mesh, in_specs=in_specs, out_specs=out_specs, check_vma=False)
```

profile of v0, /device:TPU:6, one launch (start us, length us, event | category | flops | bytes accessed | tf_op | source)
XLA Modules:
  0.0 56.3 jit_solution(12442699659803396869)
XLA Ops:
  0.6 2.0 %shard_map.94 = f32[1312,128]{1,0:T(8,128)} custom-call(f32[4,96,128]{2,1,0:T(8,128)} %bitcast.35, f32[4,32,128]{2,1,0:T(8,128)} %bitcast.38, f32[4,96,128]{2,1,0:T(8,128)} %bitcast.36, s32[4,96,128]{2,1,0:T(8,128)} %bitcast.37, s32[4,32]{1,0:T(4,128)} %bitcast.39, s32[1,32]{1,0:T(1,128)} %bitcast.40), custom_call_target="tpu_custom_call" | custom-call | tf_op jit(solution)/shard_map/pallas_call | solution.py:417
  2.6 6.1 %all-to-all-start = ((f32[32,41,1,128]{3,2,1,0:T(1,128)}), f32[32,41,1,128]{3,2,1,0:T(1,128)S(1)}, u32[]{:S(2)}, u32[]{:S(2)}) async-start(f32[32,41,1,128]{3,2,1,0:T(1,128)} %bitcast.32), calls=%async_computation | async-start | bytes 1343488 | tf_op jit(solution)/shard_map/all_to_all | solution.py:466
  8.7 2.5 %shard_map.95 = (f32[4,512,128]{2,1,0:T(8,128)S(1)}, f32[5,16,256]{2,1,0:T(8,128)S(1)}, f32[5,16,256]{2,1,0:T(8,128)S(1)}, f32[5,16,256]{2,1,0:T(8,128)S(1)}, f32[5,16,256]{2,1,0:T(8,128)S(1)}) custom-call(f32[5,16,16,256]{3,2,1,0:T(8,128)} %gas_hbm.3), custom_call_target="tpu_custom_call" | custom-call | flops 10000000 | tf_op jit(solution)/shard_map/pallas_call | solution.py:417
  11.2 15.4 %all-to-all-done = f32[32,41,1,128]{3,2,1,0:T(1,128)S(1)} async-done(((f32[32,41,1,128]{3,2,1,0:T(1,128)}), f32[32,41,1,128]{3,2,1,0:T(1,128)S(1)}, u32[]{:S(2)}, u32[]{:S(2)}) %all-to-all-start) | async-done | bytes 671776 | tf_op jit(solution)/shard_map/all_to_all | solution.py:466
  26.6 1.9 %shard_map.96 = (f32[4,128,128]{2,1,0:T(8,128)}, f32[4,128,128]{2,1,0:T(8,128)S(1)}, s32[32,128]{1,0:T(8,128)S(1)}) custom-call(f32[1312,128]{1,0:T(8,128)S(1)} %bitcast.30, f32[4,512,128]{2,1,0:T(8,128)S(1)} %get-tuple-element.13.table), custom_call_target="tpu_custom_call" | custom-call | flops 10000000 | tf_op jit(solution)/shard_map/pallas_call | solution.py:417
  28.4 3.9 %all-to-all-start.1 = ((f32[32,16,1,128]{3,2,1,0:T(1,128)}), f32[32,16,1,128]{3,2,1,0:T(1,128)S(1)}, u32[]{:S(2)}, u32[]{:S(2)}) async-start(f32[32,16,1,128]{3,2,1,0:T(1,128)} %bitcast.34), calls=%async_computation.1 | async-start | bytes 524288 | tf_op jit(solution)/shard_map/all_to_all | solution.py:507
  32.3 2.0 %collective-permute-start = (f32[5,16,256]{2,1,0:T(8,128)S(1)}, f32[5,16,256]{2,1,0:T(8,128)S(1)}, u32[]{:S(2)}, u32[]{:S(2)}) collective-permute-start(f32[5,16,256]{2,1,0:T(8,128)S(1)} %get-tuple-element.16), channel_id=1, source_target_pairs={{0,8},{8,16},{16,24},{1,9},{9,17},{17,25},{2,10},{10,18},{18,26},{... | collective-permute-start | bytes 245768 | tf_op jit(solution)/shard_map/ppermute | solution.py:485
  34.4 3.5 %collective-permute-start.1 = (f32[5,16,256]{2,1,0:T(8,128)S(1)}, f32[5,16,256]{2,1,0:T(8,128)S(1)}, u32[]{:S(2)}, u32[]{:S(2)}) collective-permute-start(f32[5,16,256]{2,1,0:T(8,128)S(1)} %get-tuple-element.17), channel_id=1, source_target_pairs={{8,0},{16,8},{24,16},{9,1},{17,9},{25,17},{10,2},{18,10},{26,18},{... | collective-permute-start | bytes 245768 | tf_op jit(solution)/shard_map/ppermute | solution.py:485
  37.9 3.4 %collective-permute-start.2 = (f32[5,16,256]{2,1,0:T(8,128)S(1)}, f32[5,16,256]{2,1,0:T(8,128)S(1)}, u32[]{:S(2)}, u32[]{:S(2)}) collective-permute-start(f32[5,16,256]{2,1,0:T(8,128)S(1)} %get-tuple-element.18), channel_id=1, source_target_pairs={{0,1},{1,2},{2,3},{3,4},{4,5},{5,6},{6,7},{8,9},{9,10},{10,11},{11... | collective-permute-start | bytes 245768 | tf_op jit(solution)/shard_map/ppermute | solution.py:485
  41.3 2.5 %collective-permute-start.3 = (f32[5,16,256]{2,1,0:T(8,128)S(1)}, f32[5,16,256]{2,1,0:T(8,128)S(1)}, u32[]{:S(2)}, u32[]{:S(2)}) collective-permute-start(f32[5,16,256]{2,1,0:T(8,128)S(1)} %get-tuple-element.19), channel_id=1, source_target_pairs={{1,0},{2,1},{3,2},{4,3},{5,4},{6,5},{7,6},{9,8},{10,9},{11,10},{12... | collective-permute-start | bytes 245768 | tf_op jit(solution)/shard_map/ppermute | solution.py:485
  43.8 0.0 collective-permute-done.from_x0
  43.8 0.0 collective-permute-done.1.from_x1
  43.8 0.5 collective-permute-done.2.from_y0
  44.3 4.3 %collective-permute-done.3.from_y1 = f32[5,16,256]{2,1,0:T(8,128)S(1)} collective-permute-done((f32[5,16,256]{2,1,0:T(8,128)S(1)}, f32[5,16,256]{2,1,0:T(8,128)S(1)}, u32[]{:S(2)}, u32[]{:S(2)}) %collective-permute-start.3) | collective-permute-done | bytes 81952 | tf_op jit(solution)/shard_map/ppermute | solution.py:485
  48.5 7.0 %shard_map.97 = f32[5,256,256]{2,1,0:T(8,128)} custom-call(s32[32,128]{1,0:T(8,128)S(1)} %get-tuple-element.14.ids_vmem, f32[1312,128]{1,0:T(8,128)S(1)} %bitcast.31, f32[4,128,128]{2,1,0:T(8,128)S(1)} %get-tuple-element.15.result, f32[5,16,16,256]{3,2,1,0:T(8,128)} %gas_hbm.3, f32[5,16,256]{2,1,0:T(8,128)S(1)} %collective-permute-done.from_x0, ...), custom_call_target="tpu_custom_call" | custom-call | flops 30000000 | tf_op jit(solution)/shard_map/pallas_call | solution.py:417
  55.5 0.0 all-to-all-done.1.result
  55.5 0.7 %shard_map.98 = (f32[32,12,1,128]{3,2,1,0:T(1,128)}, f32[32,4,1,128]{3,2,1,0:T(1,128)}) custom-call(f32[32,16,1,128]{3,2,1,0:T(1,128)S(1)} %all-to-all-done.1.result), custom_call_target="tpu_custom_call" | custom-call | tf_op jit(solution)/shard_map/pallas_call | solution.py:417
Async XLA Ops:
  2.6 23.9 %all-to-all-start = ((f32[32,41,1,128]{3,2,1,0:T(1,128)}), f32[32,41,1,128]{3,2,1,0:T(1,128)S(1)}, u32[]{:S(2)}, u32[]{:S(2)}) async-start(f32[32,41,1,128]{3,2,1,0:T(1,128)} %bitcast.32), calls=%async_computation | async-start | bytes 1343488 | tf_op jit(solution)/shard_map/all_to_all | solution.py:466
  28.4 27.1 %all-to-all-start.1 = ((f32[32,16,1,128]{3,2,1,0:T(1,128)}), f32[32,16,1,128]{3,2,1,0:T(1,128)S(1)}, u32[]{:S(2)}, u32[]{:S(2)}) async-start(f32[32,16,1,128]{3,2,1,0:T(1,128)} %bitcast.34), calls=%async_computation.1 | async-start | bytes 524288 | tf_op jit(solution)/shard_map/all_to_all | solution.py:507
  32.3 11.4 %collective-permute-start = (f32[5,16,256]{2,1,0:T(8,128)S(1)}, f32[5,16,256]{2,1,0:T(8,128)S(1)}, u32[]{:S(2)}, u32[]{:S(2)}) collective-permute-start(f32[5,16,256]{2,1,0:T(8,128)S(1)} %get-tuple-element.16), channel_id=1, source_target_pairs={{0,8},{8,16},{16,24},{1,9},{9,17},{17,25},{2,10},{10,18},{18,26},{... | collective-permute-start | bytes 245768 | tf_op jit(solution)/shard_map/ppermute | solution.py:485
  34.4 9.4 %collective-permute-start.1 = (f32[5,16,256]{2,1,0:T(8,128)S(1)}, f32[5,16,256]{2,1,0:T(8,128)S(1)}, u32[]{:S(2)}, u32[]{:S(2)}) collective-permute-start(f32[5,16,256]{2,1,0:T(8,128)S(1)} %get-tuple-element.17), channel_id=1, source_target_pairs={{8,0},{16,8},{24,16},{9,1},{17,9},{25,17},{10,2},{18,10},{26,18},{... | collective-permute-start | bytes 245768 | tf_op jit(solution)/shard_map/ppermute | solution.py:485
  37.9 6.3 %collective-permute-start.2 = (f32[5,16,256]{2,1,0:T(8,128)S(1)}, f32[5,16,256]{2,1,0:T(8,128)S(1)}, u32[]{:S(2)}, u32[]{:S(2)}) collective-permute-start(f32[5,16,256]{2,1,0:T(8,128)S(1)} %get-tuple-element.18), channel_id=1, source_target_pairs={{0,1},{1,2},{2,3},{3,4},{4,5},{5,6},{6,7},{8,9},{9,10},{10,11},{11... | collective-permute-start | bytes 245768 | tf_op jit(solution)/shard_map/ppermute | solution.py:485
  41.3 7.2 %collective-permute-start.3 = (f32[5,16,256]{2,1,0:T(8,128)S(1)}, f32[5,16,256]{2,1,0:T(8,128)S(1)}, u32[]{:S(2)}, u32[]{:S(2)}) collective-permute-start(f32[5,16,256]{2,1,0:T(8,128)S(1)} %get-tuple-element.19), channel_id=1, source_target_pairs={{1,0},{2,1},{3,2},{4,3},{5,4},{6,5},{7,6},{9,8},{10,9},{11,10},{12... | collective-permute-start | bytes 245768 | tf_op jit(solution)/shard_map/ppermute | solution.py:485
where the time goes:
time: 56.7 us; the launch traced here: 56.3 us
  starting transfers between devices  21.4 us (38%)
  waiting for transfers between devices  20.1 us (35%)
  Pallas kernels  14 us (25%)
  between operations  0.74 us (1%)
    all_to_all x1, waiting for transfers between devices, step(): lax.all_to_all(message.reshape(devices, rows, 1, LANES), SENT, split_axis...  15.4 us
    pallas_call x5, Pallas kernels, with_spaces(): return called(*values)  14 us
    ppermute x4, starting transfers between devices, shifted(): return lax.ppermute(value, axis, pairs)  11.4 us
    all_to_all x1, starting transfers between devices, step(): lax.all_to_all(message.reshape(devices, rows, 1, LANES), SENT, split_axis...  6.08 us
    ppermute x4, waiting for transfers between devices, shifted(): return lax.ppermute(value, axis, pairs)  4.74 us
    all_to_all x1, starting transfers between devices, step(): lax.all_to_all(returned.reshape(devices, capacity * FLOWS, 1, LANES), RET...  3.89 us
  transfers between devices with their start and end apart: 6, of which 3 were waited for; matrix products, arithmetic and copies ran while one was open for 0% of the time, Pallas kernels for 17%

commit v1 on v0

--- a/solution.py
+++ b/solution.py
@@ -65,8 +65,6 @@
         pltpu.make_async_copy(counts, counts_v, sems.at[1]),
     ]
     taken = []
-    for copy in small:
-        copy.start()
     for part in range(parts):
         taken.append([])
         for n, (source, held, count) in enumerate(sources):
@@ -74,6 +72,9 @@
             copy = pltpu.make_async_copy(source.at[:, place], held.at[:, place], sems.at[2 + part * 5 + n])
             copy.start()
             taken[-1].append(copy)
+        if part == 0:
+            for copy in small:
+                copy.start()
     sent = []
     for part in range(parts):
         for copy in taken[part]:
@@ -310,7 +311,7 @@
         sums = lax.dot_general(left, right, (((1,), (1,)), ((), ())), preferred_element_type=jnp.float32)
         return pl.multiple_of(tile * SUB, SUB), sums[:, :LANES] + sums[:, LANES:]
 
-    unroll = 16
+    unroll = 32
 
     def per_step(step, carry):
         made = [one(step * unroll + n) for n in range(unroll)]
@@ -484,11 +485,9 @@
         pairs = [(i, i + step) for i in range(count) if 0 <= i + step < count]
         return lax.ppermute(value, axis, pairs)
 
-    from_y0 = shifted(face_y1, "yz", 1)
-    from_y1 = shifted(face_y0, "yz", -1)
-    from_x0 = shifted(face_x1, "gx", 1)
-    from_x1 = shifted(face_x0, "gx", -1)
-    halo = (from_x0, from_x1, from_y0, from_y1)
+    halo = (
+        shifted(face_x1, "gx", 1), shifted(face_x0, "gx", -1), shifted(face_y1, "yz", 1), shifted(face_y0, "yz", -1)
+    )
     returned, result, ids = call(
         functools.partial(update_kernel, rows=rows, capacity=capacity),
         (

time: 56.7 us -> 56.2 us (level)
  transfers between devices with their start and end apart: 6 -> 6, of which waited for: 3 -> 3; matrix products, arithmetic and copies ran while one was open for 0% -> 0% of each run, Pallas kernels for 17% -> 16%
where the time goes in v1:
time: 56.2 us; the launch traced here: 55.7 us
  starting transfers between devices  21.4 us (38%)
  waiting for transfers between devices  20.1 us (36%)
  Pallas kernels  13.5 us (24%)
  between operations  0.74 us (1%)
    all_to_all x1, waiting for transfers between devices, step(): lax.all_to_all(message.reshape(devices, rows, 1, LANES), SENT, split_axis...  15.4 us
    pallas_call x5, Pallas kernels, with_spaces(): return called(*values)  13.5 us
    ppermute x4, starting transfers between devices, shifted(): return lax.ppermute(value, axis, pairs)  11.4 us
    all_to_all x1, starting transfers between devices, step(): lax.all_to_all(message.reshape(devices, rows, 1, LANES), SENT, split_axis...  6.08 us
    ppermute x4, waiting for transfers between devices, shifted(): return lax.ppermute(value, axis, pairs)  4.74 us
    all_to_all x1, starting transfers between devices, step(): lax.all_to_all(returned.reshape(devices, capacity * FLOWS, 1, LANES), RET...  3.89 us
  transfers between devices with their start and end apart: 6, of which 3 were waited for; matrix products, arithmetic and copies ran while one was open for 0% of the time, Pallas kernels for 16%

profile of v1, /device:TPU:6, one launch (start us, length us, event | category | flops | bytes accessed | tf_op | source)
XLA Modules:
  0.0 55.7 jit_solution(11087827218601203246)
XLA Ops:
  0.6 2.0 %shard_map.94 = f32[1312,128]{1,0:T(8,128)} custom-call(f32[4,96,128]{2,1,0:T(8,128)} %bitcast.35, f32[4,32,128]{2,1,0:T(8,128)} %bitcast.38, f32[4,96,128]{2,1,0:T(8,128)} %bitcast.36, s32[4,96,128]{2,1,0:T(8,128)} %bitcast.37, s32[4,32]{1,0:T(4,128)} %bitcast.39, s32[1,32]{1,0:T(1,128)} %bitcast.40), custom_call_target="tpu_custom_call" | custom-call | tf_op jit(solution)/shard_map/pallas_call | solution.py:418
  2.6 6.1 %all-to-all-start = ((f32[32,41,1,128]{3,2,1,0:T(1,128)}), f32[32,41,1,128]{3,2,1,0:T(1,128)S(1)}, u32[]{:S(2)}, u32[]{:S(2)}) async-start(f32[32,41,1,128]{3,2,1,0:T(1,128)} %bitcast.32), calls=%async_computation | async-start | bytes 1343488 | tf_op jit(solution)/shard_map/all_to_all | solution.py:467
  8.7 2.5 %shard_map.95 = (f32[4,512,128]{2,1,0:T(8,128)S(1)}, f32[5,16,256]{2,1,0:T(8,128)S(1)}, f32[5,16,256]{2,1,0:T(8,128)S(1)}, f32[5,16,256]{2,1,0:T(8,128)S(1)}, f32[5,16,256]{2,1,0:T(8,128)S(1)}) custom-call(f32[5,16,16,256]{3,2,1,0:T(8,128)} %gas_hbm.3), custom_call_target="tpu_custom_call" | custom-call | flops 10000000 | tf_op jit(solution)/shard_map/pallas_call | solution.py:418
  11.2 15.4 %all-to-all-done = f32[32,41,1,128]{3,2,1,0:T(1,128)S(1)} async-done(((f32[32,41,1,128]{3,2,1,0:T(1,128)}), f32[32,41,1,128]{3,2,1,0:T(1,128)S(1)}, u32[]{:S(2)}, u32[]{:S(2)}) %all-to-all-start) | async-done | bytes 671776 | tf_op jit(solution)/shard_map/all_to_all | solution.py:467
  26.6 1.9 %shard_map.96 = (f32[4,128,128]{2,1,0:T(8,128)}, f32[4,128,128]{2,1,0:T(8,128)S(1)}, s32[32,128]{1,0:T(8,128)S(1)}) custom-call(f32[1312,128]{1,0:T(8,128)S(1)} %bitcast.30, f32[4,512,128]{2,1,0:T(8,128)S(1)} %get-tuple-element.13.table), custom_call_target="tpu_custom_call" | custom-call | flops 10000000 | tf_op jit(solution)/shard_map/pallas_call | solution.py:418
  28.4 3.9 %all-to-all-start.1 = ((f32[32,16,1,128]{3,2,1,0:T(1,128)}), f32[32,16,1,128]{3,2,1,0:T(1,128)S(1)}, u32[]{:S(2)}, u32[]{:S(2)}) async-start(f32[32,16,1,128]{3,2,1,0:T(1,128)} %bitcast.34), calls=%async_computation.1 | async-start | bytes 524288 | tf_op jit(solution)/shard_map/all_to_all | solution.py:506
  32.4 2.0 %collective-permute-start = (f32[5,16,256]{2,1,0:T(8,128)S(1)}, f32[5,16,256]{2,1,0:T(8,128)S(1)}, u32[]{:S(2)}, u32[]{:S(2)}) collective-permute-start(f32[5,16,256]{2,1,0:T(8,128)S(1)} %get-tuple-element.16), channel_id=1, source_target_pairs={{0,8},{8,16},{16,24},{1,9},{9,17},{17,25},{2,10},{10,18},{18,26},{... | collective-permute-start | bytes 245768 | tf_op jit(solution)/shard_map/ppermute | solution.py:486
  34.4 3.5 %collective-permute-start.1 = (f32[5,16,256]{2,1,0:T(8,128)S(1)}, f32[5,16,256]{2,1,0:T(8,128)S(1)}, u32[]{:S(2)}, u32[]{:S(2)}) collective-permute-start(f32[5,16,256]{2,1,0:T(8,128)S(1)} %get-tuple-element.17), channel_id=1, source_target_pairs={{8,0},{16,8},{24,16},{9,1},{17,9},{25,17},{10,2},{18,10},{26,18},{... | collective-permute-start | bytes 245768 | tf_op jit(solution)/shard_map/ppermute | solution.py:486
  37.9 3.4 %collective-permute-start.2 = (f32[5,16,256]{2,1,0:T(8,128)S(1)}, f32[5,16,256]{2,1,0:T(8,128)S(1)}, u32[]{:S(2)}, u32[]{:S(2)}) collective-permute-start(f32[5,16,256]{2,1,0:T(8,128)S(1)} %get-tuple-element.18), channel_id=1, source_target_pairs={{0,1},{1,2},{2,3},{3,4},{4,5},{5,6},{6,7},{8,9},{9,10},{10,11},{11... | collective-permute-start | bytes 245768 | tf_op jit(solution)/shard_map/ppermute | solution.py:486
  41.3 2.5 %collective-permute-start.3 = (f32[5,16,256]{2,1,0:T(8,128)S(1)}, f32[5,16,256]{2,1,0:T(8,128)S(1)}, u32[]{:S(2)}, u32[]{:S(2)}) collective-permute-start(f32[5,16,256]{2,1,0:T(8,128)S(1)} %get-tuple-element.19), channel_id=1, source_target_pairs={{1,0},{2,1},{3,2},{4,3},{5,4},{6,5},{7,6},{9,8},{10,9},{11,10},{12... | collective-permute-start | bytes 245768 | tf_op jit(solution)/shard_map/ppermute | solution.py:486
  43.8 0.0 collective-permute-done.from_x0
  43.8 0.0 collective-permute-done.1.from_x1
  43.8 0.5 collective-permute-done.2.from_y0
  44.3 4.3 %collective-permute-done.3.from_y1 = f32[5,16,256]{2,1,0:T(8,128)S(1)} collective-permute-done((f32[5,16,256]{2,1,0:T(8,128)S(1)}, f32[5,16,256]{2,1,0:T(8,128)S(1)}, u32[]{:S(2)}, u32[]{:S(2)}) %collective-permute-start.3) | collective-permute-done | bytes 81952 | tf_op jit(solution)/shard_map/ppermute | solution.py:486
  48.5 6.5 %shard_map.97 = f32[5,256,256]{2,1,0:T(8,128)} custom-call(s32[32,128]{1,0:T(8,128)S(1)} %get-tuple-element.14.ids_vmem, f32[1312,128]{1,0:T(8,128)S(1)} %bitcast.31, f32[4,128,128]{2,1,0:T(8,128)S(1)} %get-tuple-element.15.result, f32[5,16,16,256]{3,2,1,0:T(8,128)} %gas_hbm.3, f32[5,16,256]{2,1,0:T(8,128)S(1)} %collective-permute-done.from_x0, ...), custom_call_target="tpu_custom_call" | custom-call | flops 30000000 | tf_op jit(solution)/shard_map/pallas_call | solution.py:418
  55.0 0.0 all-to-all-done.1.result
  55.0 0.7 %shard_map.98 = (f32[32,12,1,128]{3,2,1,0:T(1,128)}, f32[32,4,1,128]{3,2,1,0:T(1,128)}) custom-call(f32[32,16,1,128]{3,2,1,0:T(1,128)S(1)} %all-to-all-done.1.result), custom_call_target="tpu_custom_call" | custom-call | tf_op jit(solution)/shard_map/pallas_call | solution.py:418
Async XLA Ops:
  2.6 23.9 %all-to-all-start = ((f32[32,41,1,128]{3,2,1,0:T(1,128)}), f32[32,41,1,128]{3,2,1,0:T(1,128)S(1)}, u32[]{:S(2)}, u32[]{:S(2)}) async-start(f32[32,41,1,128]{3,2,1,0:T(1,128)} %bitcast.32), calls=%async_computation | async-start | bytes 1343488 | tf_op jit(solution)/shard_map/all_to_all | solution.py:467
  28.4 26.6 %all-to-all-start.1 = ((f32[32,16,1,128]{3,2,1,0:T(1,128)}), f32[32,16,1,128]{3,2,1,0:T(1,128)S(1)}, u32[]{:S(2)}, u32[]{:S(2)}) async-start(f32[32,16,1,128]{3,2,1,0:T(1,128)} %bitcast.34), calls=%async_computation.1 | async-start | bytes 524288 | tf_op jit(solution)/shard_map/all_to_all | solution.py:506
  32.4 11.4 %collective-permute-start = (f32[5,16,256]{2,1,0:T(8,128)S(1)}, f32[5,16,256]{2,1,0:T(8,128)S(1)}, u32[]{:S(2)}, u32[]{:S(2)}) collective-permute-start(f32[5,16,256]{2,1,0:T(8,128)S(1)} %get-tuple-element.16), channel_id=1, source_target_pairs={{0,8},{8,16},{16,24},{1,9},{9,17},{17,25},{2,10},{10,18},{18,26},{... | collective-permute-start | bytes 245768 | tf_op jit(solution)/shard_map/ppermute | solution.py:486
  34.4 9.4 %collective-permute-start.1 = (f32[5,16,256]{2,1,0:T(8,128)S(1)}, f32[5,16,256]{2,1,0:T(8,128)S(1)}, u32[]{:S(2)}, u32[]{:S(2)}) collective-permute-start(f32[5,16,256]{2,1,0:T(8,128)S(1)} %get-tuple-element.17), channel_id=1, source_target_pairs={{8,0},{16,8},{24,16},{9,1},{17,9},{25,17},{10,2},{18,10},{26,18},{... | collective-permute-start | bytes 245768 | tf_op jit(solution)/shard_map/ppermute | solution.py:486
  37.9 6.3 %collective-permute-start.2 = (f32[5,16,256]{2,1,0:T(8,128)S(1)}, f32[5,16,256]{2,1,0:T(8,128)S(1)}, u32[]{:S(2)}, u32[]{:S(2)}) collective-permute-start(f32[5,16,256]{2,1,0:T(8,128)S(1)} %get-tuple-element.18), channel_id=1, source_target_pairs={{0,1},{1,2},{2,3},{3,4},{4,5},{5,6},{6,7},{8,9},{9,10},{10,11},{11... | collective-permute-start | bytes 245768 | tf_op jit(solution)/shard_map/ppermute | solution.py:486
  41.3 7.2 %collective-permute-start.3 = (f32[5,16,256]{2,1,0:T(8,128)S(1)}, f32[5,16,256]{2,1,0:T(8,128)S(1)}, u32[]{:S(2)}, u32[]{:S(2)}) collective-permute-start(f32[5,16,256]{2,1,0:T(8,128)S(1)} %get-tuple-element.19), channel_id=1, source_target_pairs={{1,0},{2,1},{3,2},{4,3},{5,4},{6,5},{7,6},{9,8},{10,9},{11,10},{12... | collective-permute-start | bytes 245768 | tf_op jit(solution)/shard_map/ppermute | solution.py:486
